TPU v7x, 256 devices: a whole 4x4x8 slice. The times are simulated.
256 devices in a mesh: vtx: 64 (over z, y_lo, x), src: 4 (over y_hi, core).
Axes of the slice: x: 4, y: 4 (y_hi: 2, y_lo: 2; y = y_hi * 2 + y_lo), z: 8, core: 2. Of those that a mesh axis runs over, the one named last changes fastest.
Arguments:
- heat: float32 [64, 512, 8192], P(None, ('vtx', 'src')), may hold values from -12 to 12
- cotan: float32 [4, 512, 8192], P(None, 'vtx'), may hold values from 0.2 to 2
- source_index: int32 [64], replicated, may hold values from 0 to 4194303
Outputs:
- normalised: float32 [64, 512, 8192], P('src', 'vtx')
- col_norm: float32 [64], P('src')
Inputs may be any that keep to these rules, and one draw needn't show every extreme that they name: `source_index`: row-major vertex indices, sources may share a vertex.
All inputs are finite; a program needn't handle non-finite values.
Results may differ from a plain program's by a relative error of at most 0.0003.
Values sent between devices are 32-bit elements; how exact they have to be, the bound alone decides.
A program may use at most 64 MiB of HBM per device.

v0:
```python
import math
import jax
import jax.numpy as jnp
from jax import lax
from jax.sharding import PartitionSpec as P


def from_behind(value, axis, by):
    peers = lax.axis_size(axis)
    pairs = [(i, i + by) for i in range(peers) if 0 <= i + by < peers]
    return lax.ppermute(value, axis, pairs)


def extended(value, sides, width):
    for axis, dim in sides:
        peers, length = (lax.axis_size(axis), value.shape[dim])
        up = [(i, (i + 1) % peers) for i in range(peers - 1)]
        down = [(j, i) for i, j in up]
        last = lax.slice_in_dim(value, length - width, length, axis=dim)
        first = lax.slice_in_dim(value, 0, width, axis=dim)
        before = lax.ppermute(last, axis, up)
        after = lax.ppermute(first, axis, down)
        value = jnp.concatenate([before, value, after], axis=dim)
    return value


def from_everyone(value, axis):
    peers = lax.axis_size(axis)
    return lax.all_to_all(
        jnp.broadcast_to(value[None], (peers, *value.shape)), axis, 0, 0, tiled=True
    )


def taken_together(value, axis):
    everything = from_everyone(value, axis)
    return jnp.sum(everything, axis=0)


def from_right(values):
    return jnp.concatenate([values[..., 1:], jnp.zeros_like(values[..., :1])], axis=-1)


def from_left(values):
    return jnp.concatenate([jnp.zeros_like(values[..., :1]), values[..., :-1]], axis=-1)


def masked_cotan(cotan, row_start, total_rows):
    shape = cotan.shape[1:]
    rows = row_start + lax.broadcasted_iota(jnp.int32, shape, 0)
    cols = lax.broadcasted_iota(jnp.int32, shape, 1)
    inside_col = cols < shape[1] - 1
    inside_row = rows < total_rows - 1
    mass = cotan[0]
    east = jnp.where(inside_col, cotan[1], 0.0)
    north = jnp.where(inside_row, cotan[2], 0.0)
    diag = jnp.where(inside_col & inside_row, cotan[3], 0.0)
    return (mass, east, north, diag)


def stencil_defect(padded, mass, east, north_ext, diag_ext, row_start, sources, amplitude):
    center = padded[:, 1:-1, :]
    above = padded[:, 2:, :]
    below = padded[:, :-2, :]
    north = north_ext[1:]
    south_weight = north_ext[:-1]
    diag = diag_ext[1:]
    southwest_weight = from_left(diag_ext[:-1])
    west_weight = from_left(east)
    result = mass * center + east * (center - from_right(center))
    result = result + west_weight * (center - from_left(center))
    result = result + north * (center - above) + south_weight * (center - below)
    result = (
        result
        + diag * (center - from_right(above))
        + southwest_weight * (center - from_left(below))
    )
    count_rows, width = (center.shape[1], center.shape[2])
    row_ids = row_start + lax.broadcasted_iota(jnp.int32, (count_rows, width), 0)
    col_ids = lax.broadcasted_iota(jnp.int32, (count_rows, width), 1)
    flat = row_ids * width + col_ids
    delta = (flat[None, :, :] == sources[:, None, None]).astype(jnp.float32)
    return result - amplitude * delta


def on_device(heat, cotan, source_index):
    vtx_index = lax.axis_index("vtx")
    rows_dev = cotan.shape[1]
    width = cotan.shape[2]
    total_rows = rows_dev * lax.axis_size("vtx")
    amplitude = math.sqrt(total_rows * width) / 8.0
    block_start = vtx_index * rows_dev
    mass, east, north, diag = masked_cotan(cotan, block_start, total_rows)
    lower = from_behind(jnp.stack([north[-1:], diag[-1:]]), "vtx", 1)
    north_ext = jnp.concatenate([lower[0], north], axis=0)
    diag_ext = jnp.concatenate([lower[1], diag], axis=0)
    src_index = lax.axis_index("src")
    per_group = heat.shape[0] // lax.axis_size("src")
    tile = lax.all_to_all(heat, "src", split_axis=0, concat_axis=1, tiled=True)
    padded = extended(tile, (("vtx", 1),), 1)
    sources = lax.dynamic_slice_in_dim(source_index, src_index * per_group, per_group)
    defect = stencil_defect(
        padded, mass, east, north_ext, diag_ext, block_start, sources, amplitude
    )
    total = taken_together(jnp.sum(defect * defect, axis=(1, 2)), "vtx")
    norms = jnp.sqrt(total / (total_rows * width) + 1e-06)
    return (defect / norms[:, None, None], norms)


def solution(mesh):
    return jax.shard_map(
        on_device,
        mesh=mesh,
        in_specs=(P(None, ("vtx", "src"), None), P(None, "vtx", None), P()),
        out_specs=(P("src", "vtx", None), P("src")),
        check_vma=False,
    )
```

profile of v0, /device:TPU:8, one launch (start us, length us, event | category | flops | bytes accessed | tf_op | source)
XLA Modules:
  0.0 118.3 jit_solution(17329714812238578994)
XLA Ops:
  0.6 0.0 copy-start
  0.6 5.0 %all-to-all-start = ((f32[64,2,8192]{2,1,0:T(2,128)}), f32[64,2,8192]{2,1,0:T(2,128)}, u32[]{:S(2)}, u32[]{:S(2)}) async-start(f32[64,2,8192]{2,1,0:T(2,128)} %param.3), calls=%async_computation | async-start | bytes 8388608 | tf_op jit(solution)/shard_map/all_to_all | solution.py:98
  5.6 0.0 copy-start.2
  5.7 0.0 copy-done
  5.7 0.1 bitcast_select_fusion.1
  5.9 0.1 pad_maximum_fusion.1
  5.9 3.4 %collective-permute-start.1 = (f32[2,1,8192]{2,1,0:T(1,128)S(1)}, f32[2,1,8192]{2,1,0:T(1,128)S(1)}, u32[]{:S(2)}, u32[]{:S(2)}) collective-permute-start(f32[2,1,8192]{2,1,0:T(1,128)S(1)} %pad_maximum_fusion.1), channel_id=1, source_target_pairs={{0,4},{4,8},{8,12},{12,16},{16,20},{20,24},{24,28},{28,32},{32,36}... | collective-permute-start | bytes 196616 | tf_op jit(solution)/shard_map/ppermute | solution.py:11
  9.4 0.1 slice_bitcast_fusion
  9.5 0.1 iota_add_fusion
  9.6 0.0 copy-done.2
  9.6 0.1 dynamic_slice.3
  9.7 0.1 concatenate.32
  9.8 4.6 %collective-permute-done.1 = f32[2,1,8192]{2,1,0:T(1,128)S(1)} collective-permute-done((f32[2,1,8192]{2,1,0:T(1,128)S(1)}, f32[2,1,8192]{2,1,0:T(1,128)S(1)}, u32[]{:S(2)}, u32[]{:S(2)}) %collective-permute-start.1) | collective-permute-done | bytes 65568 | tf_op jit(solution)/shard_map/ppermute | solution.py:11
  14.5 0.2 select_maximum_fusion.2
  14.7 40.6 %all-to-all-done = f32[64,2,8192]{2,1,0:T(2,128)} async-done(((f32[64,2,8192]{2,1,0:T(2,128)}), f32[64,2,8192]{2,1,0:T(2,128)}, u32[]{:S(2)}, u32[]{:S(2)}) %all-to-all-start) | async-done | bytes 4194336 | tf_op jit(solution)/shard_map/all_to_all | solution.py:98
  55.3 4.6 %copy.10 = f32[4,16,2,8192]{3,1,2,0:T(8,128)S(1)} copy(f32[4,16,2,8192]{3,2,1,0:T(2,128)} %bitcast.1) | data formatting | bytes 8388608 | tf_op jit(solution)/shard_map/all_to_all | solution.py:98
  60.0 0.1 fusion.19
  60.0 4.6 %collective-permute-start = (f32[16,1,8192]{2,0,1:T(8,128)S(1)}, f32[16,1,8192]{2,0,1:T(8,128)S(1)}, u32[]{:S(2)}, u32[]{:S(2)}) collective-permute-start(f32[16,1,8192]{2,0,1:T(8,128)S(1)} %get-tuple-element.12), channel_id=1, source_target_pairs={{4,0},{8,4},{12,8},{16,12},{20,16},{24,20},{28,24},{32,28},{36,32}... | collective-permute-start | bytes 1572872 | tf_op jit(solution)/shard_map/ppermute | solution.py:22
  64.6 1.9 %collective-permute-start.2 = (f32[16,1,8192]{2,0,1:T(8,128)S(1)}, f32[16,1,8192]{2,0,1:T(8,128)S(1)}, u32[]{:S(2)}, u32[]{:S(2)}) collective-permute-start(f32[16,1,8192]{2,0,1:T(8,128)S(1)} %get-tuple-element.13), channel_id=1, source_target_pairs={{0,4},{4,8},{8,12},{12,16},{16,20},{20,24},{24,28},{28,32},{32,36}... | collective-permute-start | bytes 1572872 | tf_op jit(solution)/shard_map/ppermute | solution.py:21
  66.5 1.5 %fusion.18 = (f32[16,8,8191]{2,0,1:T(8,128)S(1)}, f32[16,8,8191]{2,0,1:T(8,128)S(1)}) fusion(f32[16,8,8192]{2,0,1:T(8,128)S(1)} %bitcast.28), kind=kLoop, calls=%fused_computation.47 | loop fusion | bytes 16775168 | tf_op jit(solution)/shard_map/slice | solution.py:40
  68.0 7.5 %collective-permute-done = f32[16,1,8192]{2,0,1:T(8,128)S(1)} collective-permute-done((f32[16,1,8192]{2,0,1:T(8,128)S(1)}, f32[16,1,8192]{2,0,1:T(8,128)S(1)}, u32[]{:S(2)}, u32[]{:S(2)}) %collective-permute-start) | collective-permute-done | bytes 524320 | tf_op jit(solution)/shard_map/ppermute | solution.py:22
  75.5 6.2 %collective-permute-done.2 = f32[16,1,8192]{2,0,1:T(8,128)S(1)} collective-permute-done((f32[16,1,8192]{2,0,1:T(8,128)S(1)}, f32[16,1,8192]{2,0,1:T(8,128)S(1)}, u32[]{:S(2)}, u32[]{:S(2)}) %collective-permute-start.2) | collective-permute-done | bytes 524320 | tf_op jit(solution)/shard_map/ppermute | solution.py:21
  81.7 7.7 %multiply_reduce_fusion = (f32[16]{0:T(128)S(1)}, f32[16,8,8192]{2,0,1:T(8,128)}) fusion(s32[16]{0:T(128)S(1)} %dynamic_slice.3, s32[8,8192]{1,0:T(8,128)S(1)} %iota_add_fusion, f32[16,8,8192]{2,0,1:T(8,128)S(1)} %bitcast.29, f32[16,1,8192]{2,0,1:T(8,128)S(1)} %collective-permute-done.2, f32[8,8192]{1,0:T(8,128)S(1)} %get-tuple-element.26, ...), kind=kLoop, calls=%fused_computation.23 | loop fusion | flops 35651568 | bytes 19922048 | tf_op jit(solution)/shard_map/reduce_sum | solution.py:104
  89.4 21.6 %all_to_all.24 = f32[64,1,16]{2,1,0:T(1,128)S(1)} all-to-all(f32[64,1,16]{2,1,0:T(1,128)S(1)} %broadcast_in_dim.12), channel_id=1, replica_groups=mesh['vtx'=64,'src'=4] {'vtx'}, dimensions={0} | all-to-all | bytes 8192 | tf_op jit(solution)/shard_map/all_to_all | solution.py:29
  111.0 0.1 reduce_sum.19
  111.1 0.0 copy-start.1
  111.1 2.7 %broadcast_divide_fusion = f32[16,8,8192]{2,0,1:T(8,128)S(1)} fusion(f32[16,8,8192]{2,0,1:T(8,128)} %get-tuple-element.9, f32[16]{0:T(128)S(1)} %add_sqrt_fusion), kind=kLoop, calls=%fused_computation.24 | loop fusion | flops 1048576 | bytes 8388672 | tf_op jit(solution)/shard_map/div | solution.py:106
  113.9 0.0 copy-done.1
  113.9 4.4 %copy.12 = f32[16,8,8192]{2,1,0:T(8,128)} copy(f32[16,8,8192]{2,0,1:T(8,128)S(1)} %broadcast_divide_fusion) | data formatting | bytes 8388608
  (9 shorter events, 0.2 us)
Async XLA Ops:
  0.6 5.0 %copy-start = (f32[4,8,8192]{2,1,0:T(8,128)S(1)}, f32[4,8,8192]{2,1,0:T(8,128)}, u32[]{:S(2)}) copy-start(f32[4,8,8192]{2,1,0:T(8,128)} %param.4) | copy-start | bytes 3145732
  0.6 54.7 %all-to-all-start = ((f32[64,2,8192]{2,1,0:T(2,128)}), f32[64,2,8192]{2,1,0:T(2,128)}, u32[]{:S(2)}, u32[]{:S(2)}) async-start(f32[64,2,8192]{2,1,0:T(2,128)} %param.3), calls=%async_computation | async-start | bytes 8388608 | tf_op jit(solution)/shard_map/all_to_all | solution.py:98
  5.6 4.0 %copy-start.2 = (s32[64]{0:T(128)S(1)}, s32[64]{0:T(128)}, u32[]{:S(2)}) copy-start(s32[64]{0:T(128)} %param.5) | copy-start | bytes 772
  5.9 8.5 %collective-permute-start.1 = (f32[2,1,8192]{2,1,0:T(1,128)S(1)}, f32[2,1,8192]{2,1,0:T(1,128)S(1)}, u32[]{:S(2)}, u32[]{:S(2)}) collective-permute-start(f32[2,1,8192]{2,1,0:T(1,128)S(1)} %pad_maximum_fusion.1), channel_id=1, source_target_pairs={{0,4},{4,8},{8,12},{12,16},{16,20},{20,24},{24,28},{28,32},{32,36}... | collective-permute-start | bytes 196616 | tf_op jit(solution)/shard_map/ppermute | solution.py:11
  60.0 15.4 %collective-permute-start = (f32[16,1,8192]{2,0,1:T(8,128)S(1)}, f32[16,1,8192]{2,0,1:T(8,128)S(1)}, u32[]{:S(2)}, u32[]{:S(2)}) collective-permute-start(f32[16,1,8192]{2,0,1:T(8,128)S(1)} %get-tuple-element.12), channel_id=1, source_target_pairs={{4,0},{8,4},{12,8},{16,12},{20,16},{24,20},{28,24},{32,28},{36,32}... | collective-permute-start | bytes 1572872 | tf_op jit(solution)/shard_map/ppermute | solution.py:22
  64.6 17.1 %collective-permute-start.2 = (f32[16,1,8192]{2,0,1:T(8,128)S(1)}, f32[16,1,8192]{2,0,1:T(8,128)S(1)}, u32[]{:S(2)}, u32[]{:S(2)}) collective-permute-start(f32[16,1,8192]{2,0,1:T(8,128)S(1)} %get-tuple-element.13), channel_id=1, source_target_pairs={{0,4},{4,8},{8,12},{12,16},{16,20},{20,24},{24,28},{28,32},{32,36}... | collective-permute-start | bytes 1572872 | tf_op jit(solution)/shard_map/ppermute | solution.py:21
  111.1 2.7 %copy-start.1 = (f32[16]{0:T(128)}, f32[16]{0:T(128)S(1)}, u32[]{:S(2)}) copy-start(f32[16]{0:T(128)S(1)} %add_sqrt_fusion) | copy-start | bytes 196
where the time goes:
time: 119 us; the launch traced here: 118 us
  waiting for transfers between devices  59 us (50%)
  blocking collectives  21.6 us (18%)
  starting transfers between devices  14.8 us (12%)
  other arithmetic  11.2 us (9%)
  local copies, waits for them, and re-layouts  10.9 us (9%)
    all_to_all x1, waiting for transfers between devices, on_device(): tile = lax.all_to_all(heat, 'src', split_axis=0, concat_axis=1, tiled=True)  40.6 us
    all_to_all x1, blocking collectives, from_everyone(): lax.all_to_all(jnp.broadcast_to(value[None], (peers, *value.shape)), axis...  21.6 us
    reduce_sum x1, other arithmetic, on_device(): total = taken_together(jnp.sum(defect * defect, axis=(1, 2)), 'vtx')  7.69 us
    ppermute x1, waiting for transfers between devices, extended(): after = lax.ppermute(first, axis, down)  7.47 us
    ppermute x1, waiting for transfers between devices, extended(): before = lax.ppermute(last, axis, up)  6.23 us
    all_to_all x1, starting transfers between devices, on_device(): tile = lax.all_to_all(heat, 'src', split_axis=0, concat_axis=1, tiled=True)  4.97 us
    ppermute x1, waiting for transfers between devices, from_behind(): return lax.ppermute(value, axis, pairs)  4.64 us
    all_to_all x1, local copies, waits for them, and re-layouts, on_device(): tile = lax.all_to_all(heat, 'src', split_axis=0, concat_axis=1, tiled=True)  4.62 us
  transfers between devices with their start and end apart: 4, of which 4 were waited for; matrix products, arithmetic and copies ran while one was open for 2% of the time, Pallas kernels for 0%

commit v1 on v0

--- a/solution.py
+++ b/solution.py
@@ -95,7 +95,10 @@
     diag_ext = jnp.concatenate([lower[1], diag], axis=0)
     src_index = lax.axis_index("src")
     per_group = heat.shape[0] // lax.axis_size("src")
-    tile = lax.all_to_all(heat, "src", split_axis=0, concat_axis=1, tiled=True)
+    tile = jnp.concatenate(
+        lax.all_to_all(jnp.stack(jnp.split(heat, lax.axis_size("src"), axis=0)), "src", 0, 0),
+        axis=1,
+    )
     padded = extended(tile, (("vtx", 1),), 1)
     sources = lax.dynamic_slice_in_dim(source_index, src_index * per_group, per_group)
     defect = stencil_defect(

time: 119 us -> 131 us (1.10)
  other arithmetic: 11.2 us -> 15.8 us
  waiting for transfers between devices: 59 us -> 62.7 us
  local copies, waits for them, and re-layouts: 10.9 us -> 13.6 us
  blocking collectives: 21.6 us -> 23.1 us
    all_to_all x1, waiting for transfers between devices: 40.6 us -> 49 us  [on_device(): lax.all_to_all(jnp.stack(jnp.split(heat, lax.axis_size('src'), axis=0)),...]
    ppermute x1, waiting for transfers between devices: 4.64 us -> 0.01 us  [from_behind(): return lax.ppermute(value, axis, pairs)]
    reshape x0 -> x1, local copies, waits for them, and re-layouts: none -> 4.62 us  [on_device(): jnp.concatenate(lax.all_to_all(jnp.stack(jnp.split(heat, lax.axis_size('s...]
    all_to_all x1 -> x0, local copies, waits for them, and re-layouts: 4.62 us -> none  [on_device(): tile = lax.all_to_all(heat, 'src', split_axis=0, concat_axis=1, tiled=True)]
    another operation x0 -> x1, other arithmetic: none -> 3.6 us  [on_device(): jnp.stack(jnp.split(heat, lax.axis_size('src'), axis=0))]
    another operation x0 -> x1, local copies, waits for them, and re-layouts: none -> 2.66 us  [on_device(): jnp.stack(jnp.split(heat, lax.axis_size('src'), axis=0))]
    all_to_all x1, blocking collectives: 21.6 us -> 23.1 us  [from_everyone(): lax.all_to_all(jnp.broadcast_to(value[None], (peers, *value.shape)), axis...]
  transfers between devices with their start and end apart: 4 -> 4, of which waited for: 4 -> 3; matrix products, arithmetic and copies ran while one was open for 2% -> 6% of each run, Pallas kernels for 0% -> 0%
where the time goes in v1:
time: 131 us
  waiting for transfers between devices  62.7 us (48%)
  blocking collectives  23.1 us (18%)
  other arithmetic  15.8 us (12%)
  starting transfers between devices  14.8 us (11%)
  local copies, waits for them, and re-layouts  13.6 us (10%)
    all_to_all x1, waiting for transfers between devices, on_device(): lax.all_to_all(jnp.stack(jnp.split(heat, lax.axis_size('src'), axis=0)),...  49 us
    all_to_all x1, blocking collectives, from_everyone(): lax.all_to_all(jnp.broadcast_to(value[None], (peers, *value.shape)), axis...  23.1 us
    reduce_sum x1, other arithmetic, on_device(): total = taken_together(jnp.sum(defect * defect, axis=(1, 2)), 'vtx')  7.69 us
    ppermute x1, waiting for transfers between devices, extended(): after = lax.ppermute(first, axis, down)  7.47 us
    ppermute x1, waiting for transfers between devices, extended(): before = lax.ppermute(last, axis, up)  6.23 us
    all_to_all x1, starting transfers between devices, on_device(): lax.all_to_all(jnp.stack(jnp.split(heat, lax.axis_size('src'), axis=0)),...  4.98 us
    reshape x1, local copies, waits for them, and re-layouts, on_device(): jnp.concatenate(lax.all_to_all(jnp.stack(jnp.split(heat, lax.axis_size('s...  4.62 us
    ppermute x1, starting transfers between devices, extended(): after = lax.ppermute(first, axis, down)  4.55 us
  transfers between devices with their start and end apart: 4, of which 3 were waited for; matrix products, arithmetic and copies ran while one was open for 6% of the time, Pallas kernels for 0%

profile of v1, /device:TPU:8, one launch (start us, length us, event | category | flops | bytes accessed | tf_op | source)
XLA Modules:
  0.0 130.8 jit_solution(152906078681971270)
XLA Ops:
  0.7 1.1 bitcast_select_fusion.1
  1.9 0.1 pad_maximum_fusion.2
  2.0 3.4 %collective-permute-start.1 = (f32[2,1,8192]{2,1,0:T(1,128)S(1)}, f32[2,1,8192]{2,1,0:T(1,128)S(1)}, u32[]{:S(2)}, u32[]{:S(2)}) collective-permute-start(f32[2,1,8192]{2,1,0:T(1,128)S(1)} %pad_maximum_fusion.2), channel_id=1, source_target_pairs={{0,4},{4,8},{8,12},{12,16},{16,20},{20,24},{24,28},{28,32},{32,36}... | collective-permute-start | bytes 196616 | tf_op jit(solution)/shard_map/ppermute | solution.py:11
  5.4 2.7 %slice_bitcast_fusion.3 = (f32[1,16,2,8192]{3,2,1,0:T(2,128)S(1)}, f32[1,16,2,8192]{3,2,1,0:T(2,128)S(1)}, f32[1,16,2,8192]{3,2,1,0:T(2,128)S(1)}, f32[1,16,2,8192]{3,2,1,0:T(2,128)S(1)}) fusion(f32[64,2,8192]{2,1,0:T(2,128)} %param.3), kind=kLoop, calls=%fused_computation.29 | loop fusion | bytes 8388608 | tf_op jit(solution)/shard_map/stack | solution.py:99
  8.0 3.6 %pad_maximum_fusion = f32[4,16,2,8192]{3,2,1,0:T(2,128)} fusion(f32[1,16,2,8192]{3,2,1,0:T(2,128)S(1)} %get-tuple-element.16, f32[1,16,2,8192]{3,2,1,0:T(2,128)S(1)} %get-tuple-element.17, f32[1,16,2,8192]{3,2,1,0:T(2,128)S(1)} %get-tuple-element.15, f32[1,16,2,8192]{3,2,1,0:T(2,128)S(1)} %get-tuple-element.14), kind=kLoop, calls=%fused_computation.23 | loop fusion | flops 3145728 | bytes 8388608 | tf_op jit(solution)/shard_map/stack | solution.py:99
  11.6 0.0 copy-start
  11.6 0.0 copy-start.2
  11.6 5.0 %all-to-all-start = ((f32[4,16,2,8192]{3,2,1,0:T(2,128)}), f32[4,16,2,8192]{3,2,1,0:T(2,128)}, u32[]{:S(2)}, u32[]{:S(2)}) async-start(f32[4,16,2,8192]{3,2,1,0:T(2,128)} %pad_maximum_fusion), calls=%async_computation | async-start | bytes 8388608 | tf_op jit(solution)/shard_map/all_to_all | solution.py:99
  16.6 0.0 copy-done
  16.6 0.1 slice_bitcast_fusion.4
  16.8 0.1 iota_add_fusion
  16.9 0.0 copy-done.2
  16.9 0.1 dynamic_slice.3
  17.0 0.1 concatenate.32
  17.1 0.0 collective-permute-done.1
  17.2 0.2 select_maximum_fusion.2
  17.4 49.0 %all-to-all-done = f32[4,16,2,8192]{3,2,1,0:T(2,128)} async-done(((f32[4,16,2,8192]{3,2,1,0:T(2,128)}), f32[4,16,2,8192]{3,2,1,0:T(2,128)}, u32[]{:S(2)}, u32[]{:S(2)}) %all-to-all-start) | async-done | bytes 4194336 | tf_op jit(solution)/shard_map/all_to_all | solution.py:99
  66.3 4.6 %copy.10 = f32[16,4,2,8192]{3,0,2,1:T(8,128)S(1)} copy(f32[16,4,2,8192]{3,2,0,1:T(2,128)} %bitcast.5) | data formatting | bytes 8388608 | tf_op jit(solution)/shard_map/reshape | solution.py:98
  71.0 0.1 fusion.19
  71.0 4.6 %collective-permute-start = (f32[16,1,8192]{2,0,1:T(8,128)S(1)}, f32[16,1,8192]{2,0,1:T(8,128)S(1)}, u32[]{:S(2)}, u32[]{:S(2)}) collective-permute-start(f32[16,1,8192]{2,0,1:T(8,128)S(1)} %get-tuple-element.12), channel_id=1, source_target_pairs={{4,0},{8,4},{12,8},{16,12},{20,16},{24,20},{28,24},{32,28},{36,32}... | collective-permute-start | bytes 1572872 | tf_op jit(solution)/shard_map/ppermute | solution.py:22
  75.6 1.9 %collective-permute-start.2 = (f32[16,1,8192]{2,0,1:T(8,128)S(1)}, f32[16,1,8192]{2,0,1:T(8,128)S(1)}, u32[]{:S(2)}, u32[]{:S(2)}) collective-permute-start(f32[16,1,8192]{2,0,1:T(8,128)S(1)} %get-tuple-element.13), channel_id=1, source_target_pairs={{0,4},{4,8},{8,12},{12,16},{16,20},{20,24},{24,28},{28,32},{32,36}... | collective-permute-start | bytes 1572872 | tf_op jit(solution)/shard_map/ppermute | solution.py:21
  77.5 1.5 %fusion.18 = (f32[16,8,8191]{2,0,1:T(8,128)S(1)}, f32[16,8,8191]{2,0,1:T(8,128)S(1)}) fusion(f32[16,8,8192]{2,0,1:T(8,128)S(1)} %bitcast.34), kind=kLoop, calls=%fused_computation.52 | loop fusion | bytes 16775168 | tf_op jit(solution)/shard_map/slice | solution.py:40
  79.0 7.5 %collective-permute-done = f32[16,1,8192]{2,0,1:T(8,128)S(1)} collective-permute-done((f32[16,1,8192]{2,0,1:T(8,128)S(1)}, f32[16,1,8192]{2,0,1:T(8,128)S(1)}, u32[]{:S(2)}, u32[]{:S(2)}) %collective-permute-start) | collective-permute-done | bytes 524320 | tf_op jit(solution)/shard_map/ppermute | solution.py:22
  86.5 6.2 %collective-permute-done.2 = f32[16,1,8192]{2,0,1:T(8,128)S(1)} collective-permute-done((f32[16,1,8192]{2,0,1:T(8,128)S(1)}, f32[16,1,8192]{2,0,1:T(8,128)S(1)}, u32[]{:S(2)}, u32[]{:S(2)}) %collective-permute-start.2) | collective-permute-done | bytes 524320 | tf_op jit(solution)/shard_map/ppermute | solution.py:21
  92.7 7.7 %multiply_reduce_fusion = (f32[16]{0:T(128)S(1)}, f32[16,8,8192]{2,0,1:T(8,128)}) fusion(s32[16]{0:T(128)S(1)} %dynamic_slice.3, s32[8,8192]{1,0:T(8,128)S(1)} %iota_add_fusion, f32[16,8,8192]{2,0,1:T(8,128)S(1)} %bitcast.35, f32[16,1,8192]{2,0,1:T(8,128)S(1)} %collective-permute-done.2, f32[8,8192]{1,0:T(8,128)S(1)} %get-tuple-element.30, ...), kind=kLoop, calls=%fused_computation.24 | loop fusion | flops 35651568 | bytes 19922048 | tf_op jit(solution)/shard_map/reduce_sum | solution.py:107
  100.4 23.1 %all_to_all.11 = f32[64,1,16]{2,1,0:T(1,128)S(1)} all-to-all(f32[64,1,16]{2,1,0:T(1,128)S(1)} %broadcast_in_dim.12), channel_id=1, replica_groups=mesh['vtx'=64,'src'=4] {'vtx'}, dimensions={0} | all-to-all | bytes 8192 | tf_op jit(solution)/shard_map/all_to_all | solution.py:29
  123.5 0.1 reduce_sum.19
  123.6 0.0 copy-start.1
  123.6 2.7 %broadcast_divide_fusion = f32[16,8,8192]{2,0,1:T(8,128)S(1)} fusion(f32[16,8,8192]{2,0,1:T(8,128)} %get-tuple-element.9, f32[16]{0:T(128)S(1)} %add_sqrt_fusion), kind=kLoop, calls=%fused_computation.25 | loop fusion | flops 1048576 | bytes 8388672 | tf_op jit(solution)/shard_map/div | solution.py:109
  126.3 0.0 copy-done.1
  126.3 4.4 %copy.12 = f32[16,8,8192]{2,1,0:T(8,128)} copy(f32[16,8,8192]{2,0,1:T(8,128)S(1)} %broadcast_divide_fusion) | data formatting | bytes 8388608
  (9 shorter events, 0.2 us)
Async XLA Ops:
  2.0 15.2 %collective-permute-start.1 = (f32[2,1,8192]{2,1,0:T(1,128)S(1)}, f32[2,1,8192]{2,1,0:T(1,128)S(1)}, u32[]{:S(2)}, u32[]{:S(2)}) collective-permute-start(f32[2,1,8192]{2,1,0:T(1,128)S(1)} %pad_maximum_fusion.2), channel_id=1, source_target_pairs={{0,4},{4,8},{8,12},{12,16},{16,20},{20,24},{24,28},{28,32},{32,36}... | collective-permute-start | bytes 196616 | tf_op jit(solution)/shard_map/ppermute | solution.py:11
  11.6 5.0 %copy-start = (f32[4,8,8192]{2,1,0:T(8,128)S(1)}, f32[4,8,8192]{2,1,0:T(8,128)}, u32[]{:S(2)}) copy-start(f32[4,8,8192]{2,1,0:T(8,128)} %param.4) | copy-start | bytes 3145732
  11.6 5.3 %copy-start.2 = (s32[64]{0:T(128)S(1)}, s32[64]{0:T(128)}, u32[]{:S(2)}) copy-start(s32[64]{0:T(128)} %param.5) | copy-start | bytes 772
  11.6 54.7 %all-to-all-start = ((f32[4,16,2,8192]{3,2,1,0:T(2,128)}), f32[4,16,2,8192]{3,2,1,0:T(2,128)}, u32[]{:S(2)}, u32[]{:S(2)}) async-start(f32[4,16,2,8192]{3,2,1,0:T(2,128)} %pad_maximum_fusion), calls=%async_computation | async-start | bytes 8388608 | tf_op jit(solution)/shard_map/all_to_all | solution.py:99
  71.0 15.4 %collective-permute-start = (f32[16,1,8192]{2,0,1:T(8,128)S(1)}, f32[16,1,8192]{2,0,1:T(8,128)S(1)}, u32[]{:S(2)}, u32[]{:S(2)}) collective-permute-start(f32[16,1,8192]{2,0,1:T(8,128)S(1)} %get-tuple-element.12), channel_id=1, source_target_pairs={{4,0},{8,4},{12,8},{16,12},{20,16},{24,20},{28,24},{32,28},{36,32}... | collective-permute-start | bytes 1572872 | tf_op jit(solution)/shard_map/ppermute | solution.py:22
  75.6 17.1 %collective-permute-start.2 = (f32[16,1,8192]{2,0,1:T(8,128)S(1)}, f32[16,1,8192]{2,0,1:T(8,128)S(1)}, u32[]{:S(2)}, u32[]{:S(2)}) collective-permute-start(f32[16,1,8192]{2,0,1:T(8,128)S(1)} %get-tuple-element.13), channel_id=1, source_target_pairs={{0,4},{4,8},{8,12},{12,16},{16,20},{20,24},{24,28},{28,32},{32,36}... | collective-permute-start | bytes 1572872 | tf_op jit(solution)/shard_map/ppermute | solution.py:21
  123.6 2.7 %copy-start.1 = (f32[16]{0:T(128)}, f32[16]{0:T(128)S(1)}, u32[]{:S(2)}) copy-start(f32[16]{0:T(128)S(1)} %add_sqrt_fusion) | copy-start | bytes 196
